TPU v7x, 32 devices: a whole 2x2x4 slice. The times are simulated.
32 devices in a mesh: vp: 8 (over z, y), rep: 4 (over x, core).
Axes of the slice: x: 2, y: 2, z: 4, core: 2. Of those that a mesh axis runs over, the one named last changes fastest.
Arguments:
- features: bfloat16 [65536, 256], P(('vp', 'rep')), may hold values from -48 to 48
- tile_values: bfloat16 [8192, 128, 128], P(('vp', 'rep')), may hold values from 0 to 0.0014648438
- tile_cols: int32 [8192], P(('vp', 'rep')), may hold values from 0 to 31, as said below
- halo_rows: int32 [32, 4, 4], P(('vp', 'rep')), may hold values from 0 to 15
Outputs:
- scores: bfloat16 [65536, 256], P(('vp', 'rep'))
Inputs may be any that keep to these rules, and one draw needn't show every extreme that they name: `tile_cols`: values below 16 name one of the shard's own row blocks; value 16 + o * 4 + j names the j-th block sent by peer o. Every value occurs on every shard.
All inputs are finite; a program needn't handle non-finite values.
Results may differ from a plain program's by a relative error of at most 0.002.
Values may be sent and summed in bfloat16 or wider, within the bound.
A program may use at most 128 MiB of HBM per device.

v0:
```python
import jax
import jax.numpy as jnp
from jax import lax
from jax.sharding import PartitionSpec as P

ITERS = 3


peer_offsets = (1, -1, 4, -4)


def passed_along(shard, axis, by):
    count = lax.axis_size(axis)
    return lax.ppermute(shard, axis, [(i, (i + by) % count) for i in range(count)])


def local(features, tile_values, tile_cols, halo_rows):
    tile_size = tile_values.shape[1]
    classes = features.shape[1]
    nblocks = features.shape[0] // tile_size
    per_row = tile_values.shape[0] // nblocks
    shards = lax.axis_size("vp") * lax.axis_size("rep")
    vertices = features.shape[0] * shards
    send_lists = halo_rows[0]
    tiles = tile_values.reshape(nblocks, per_row, tile_size, tile_size)
    tile_slots = tile_cols.reshape(nblocks, per_row)
    current = features
    for iteration in range(ITERS):
        own_blocks = current.reshape(nblocks, tile_size, classes)
        halo_blocks = []
        for which in range(4):
            halo_blocks.append(
                passed_along(own_blocks[send_lists[which]], ("vp", "rep"), peer_offsets[which])
            )
        block_table = jnp.concatenate([own_blocks] + halo_blocks, axis=0)
        picked = block_table[tile_slots]
        propagated = jnp.einsum(
            "rtij,rtjc->ric", tiles, picked, preferred_element_type=jnp.float32
        ).reshape(-1, classes)
        blended = 0.9 * propagated + 0.1 * features.astype(jnp.float32)
        local_mass = jnp.sum(blended * blended, axis=0)
        total_mass = lax.psum(local_mass, ("vp", "rep"))
        current = (blended / jnp.sqrt(0.05 + total_mass / vertices)).astype(jnp.bfloat16)
    return current


def solution(mesh):
    return jax.shard_map(
        local,
        mesh=mesh,
        in_specs=(
            P(("vp", "rep"), None),
            P(("vp", "rep"), None, None),
            P(("vp", "rep")),
            P(("vp", "rep"), None, None),
        ),
        out_specs=P(("vp", "rep"), None),
        check_vma=False,
    )
```

profile of v0, /device:TPU:0, one launch (start us, length us, event | category | flops | bytes accessed | tf_op | source)
XLA Modules:
  0.0 266.9 jit_solution(13147094693537022093)
XLA Ops:
  2.6 6.1 %collective-permute-start.3 = (bf16[4,128,256]{2,1,0:T(8,128)(2,1)S(1)}, bf16[4,128,256]{2,1,0:T(8,128)(2,1)}, u32[]{:S(2)}, u32[]{:S(2)}) collective-permute-start(bf16[4,128,256]{2,1,0:T(8,128)(2,1)S(1)} %gather_fusion.3), channel_id=1, source_target_pairs={{0,28},{1,29},{2,30},{3,31},{4,0},{5,1},{6,2},{7,3},{8,4},{9,5},{1... | collective-permute-start | bytes 786440 | tf_op jit(solution)/shard_map/ppermute | solution.py:14
  8.7 2.5 gather_fusion.1
  11.8 2.5 gather_fusion
  14.3 2.5 gather_fusion.2
  18.6 6.0 %collective-permute-done = bf16[4,128,256]{2,1,0:T(8,128)(2,1)} collective-permute-done((bf16[4,128,256]{2,1,0:T(8,128)(2,1)}, bf16[4,128,256]{2,1,0:T(8,128)(2,1)}, u32[]{:S(2)}, u32[]{:S(2)}) %collective-permute-start) | collective-permute-done | bytes 262176 | tf_op jit(solution)/shard_map/ppermute | solution.py:14
  26.6 3.0 %collective-permute-done.2 = bf16[4,128,256]{2,1,0:T(8,128)(2,1)} collective-permute-done((bf16[4,128,256]{2,1,0:T(8,128)(2,1)}, bf16[4,128,256]{2,1,0:T(8,128)(2,1)}, u32[]{:S(2)}, u32[]{:S(2)}) %collective-permute-start.2) | collective-permute-done | bytes 262176 | tf_op jit(solution)/shard_map/ppermute | solution.py:14
  31.6 9.7 %gather_fusion.4 = bf16[256,128,256]{2,1,0:T(8,128)(2,1)} fusion(bf16[32,128,256]{2,1,0:T(8,128)(2,1)S(1)} %constant_dynamic-update-slice_fusion, s32[1024]{0:T(1024)S(1)} %pad_clamp_fusion), kind=kCustom, calls=%fused_computation.4 | custom fusion | bytes 33555456 | tf_op jit(solution)/shard_map/gather | solution.py:36
  41.3 10.5 %bitcast_multiply_fusion.2 = f32[16,256,128]{1,2,0:T(8,128)S(1)} fusion(bf16[16,16,128,128]{3,2,1,0:T(8,128)(2,1)} %bitcast.64, bf16[16,16,128,256]{3,2,1,0:T(8,128)(2,1)} %bitcast.68), kind=kOutput, calls=%fused_computation.20 | convolution fusion | flops 2148007936 | bytes 27262976 | tf_op jit(solution)/shard_map/rtij,rtjc->ric/dot_general | solution.py:37
  52.2 36.8 %psum.21 = f32[256]{0:T(256)S(1)} all-reduce(f32[256]{0:T(256)S(1)} %multiply_reduce_fusion.2), channel_id=1, replica_groups=mesh['vp'=8,'rep'=4] {'vp','rep'}, use_global_device_ids=true, to_apply=%region_1.0 | all-reduce | flops 256 | bytes 2048 | tf_op jit(solution)/shard_map/psum | solution.py:42
  92.9 2.5 gather_fusion.6
  95.3 5.3 %collective-permute-start.5 = (bf16[4,128,256]{2,1,0:T(8,128)(2,1)}, bf16[4,128,256]{2,1,0:T(8,128)(2,1)}, u32[]{:S(2)}, u32[]{:S(2)}) collective-permute-start(bf16[4,128,256]{2,1,0:T(8,128)(2,1)} %gather_fusion.6), channel_id=1, source_target_pairs={{0,31},{1,0},{2,1},{3,2},{4,3},{5,4},{6,5},{7,6},{8,7},{9,8},{10,9... | collective-permute-start | bytes 786440 | tf_op jit(solution)/shard_map/ppermute | solution.py:14
  100.7 2.5 gather_fusion.7
  106.3 4.8 %collective-permute-start.7 = (bf16[4,128,256]{2,1,0:T(8,128)(2,1)S(1)}, bf16[4,128,256]{2,1,0:T(8,128)(2,1)S(1)}, u32[]{:S(2)}, u32[]{:S(2)}) collective-permute-start(bf16[4,128,256]{2,1,0:T(8,128)(2,1)S(1)} %gather_fusion.8), channel_id=1, source_target_pairs={{0,28},{1,29},{2,30},{3,31},{4,0},{5,1},{6,2},{7,3},{8,4},{9,5},{1... | collective-permute-start | bytes 786440 | tf_op jit(solution)/shard_map/ppermute | solution.py:14
  114.0 3.0 %collective-permute-done.7 = bf16[4,128,256]{2,1,0:T(8,128)(2,1)S(1)} collective-permute-done((bf16[4,128,256]{2,1,0:T(8,128)(2,1)S(1)}, bf16[4,128,256]{2,1,0:T(8,128)(2,1)S(1)}, u32[]{:S(2)}, u32[]{:S(2)}) %collective-permute-start.7) | collective-permute-done | bytes 262176 | tf_op jit(solution)/shard_map/ppermute | solution.py:14
  117.0 9.7 %gather_fusion.9 = bf16[256,128,256]{2,1,0:T(8,128)(2,1)} fusion(bf16[32,128,256]{2,1,0:T(8,128)(2,1)S(1)} %constant_dynamic-update-slice_fusion.5, s32[1024]{0:T(1024)S(1)} %pad_clamp_fusion), kind=kCustom, calls=%fused_computation.9 | custom fusion | bytes 33555456 | tf_op jit(solution)/shard_map/gather | solution.py:36
  126.7 10.5 %bitcast_multiply_fusion.1 = f32[16,256,128]{1,2,0:T(8,128)S(1)} fusion(bf16[16,16,128,128]{3,2,1,0:T(8,128)(2,1)} %bitcast.65, bf16[16,16,128,256]{3,2,1,0:T(8,128)(2,1)} %bitcast.69), kind=kOutput, calls=%fused_computation.19 | convolution fusion | flops 2148007936 | bytes 27262976 | tf_op jit(solution)/shard_map/rtij,rtjc->ric/dot_general | solution.py:37
  137.7 41.1 %psum.22 = f32[256]{0:T(256)S(1)} all-reduce(f32[256]{0:T(256)S(1)} %multiply_reduce_fusion.1), channel_id=1, replica_groups=mesh['vp'=8,'rep'=4] {'vp','rep'}, use_global_device_ids=true, to_apply=%region_3.0 | all-reduce | flops 256 | bytes 2048 | tf_op jit(solution)/shard_map/psum | solution.py:42
  182.5 2.5 gather_fusion.11
  185.0 5.3 %collective-permute-start.9 = (bf16[4,128,256]{2,1,0:T(8,128)(2,1)}, bf16[4,128,256]{2,1,0:T(8,128)(2,1)}, u32[]{:S(2)}, u32[]{:S(2)}) collective-permute-start(bf16[4,128,256]{2,1,0:T(8,128)(2,1)} %gather_fusion.11), channel_id=1, source_target_pairs={{0,31},{1,0},{2,1},{3,2},{4,3},{5,4},{6,5},{7,6},{8,7},{9,8},{10,9... | collective-permute-start | bytes 786440 | tf_op jit(solution)/shard_map/ppermute | solution.py:14
  193.5 2.5 gather_fusion.13
  196.0 4.7 %collective-permute-start.11 = (bf16[4,128,256]{2,1,0:T(8,128)(2,1)}, bf16[4,128,256]{2,1,0:T(8,128)(2,1)S(1)}, u32[]{:S(2)}, u32[]{:S(2)}) collective-permute-start(bf16[4,128,256]{2,1,0:T(8,128)(2,1)} %gather_fusion.13), channel_id=1, source_target_pairs={{0,28},{1,29},{2,30},{3,31},{4,0},{5,1},{6,2},{7,3},{8,4},{9,5},{1... | collective-permute-start | bytes 786440 | tf_op jit(solution)/shard_map/ppermute | solution.py:14
  205.8 9.7 %gather_fusion.14 = bf16[256,128,256]{2,1,0:T(8,128)(2,1)} fusion(bf16[32,128,256]{2,1,0:T(8,128)(2,1)S(1)} %constant_dynamic-update-slice_fusion.10, s32[1024]{0:T(1024)S(1)} %pad_clamp_fusion), kind=kCustom, calls=%fused_computation.14 | custom fusion | bytes 33555456 | tf_op jit(solution)/shard_map/gather | solution.py:36
  215.5 10.5 %bitcast_multiply_fusion = f32[16,256,128]{1,2,0:T(8,128)S(1)} fusion(bf16[16,16,128,128]{3,2,1,0:T(8,128)(2,1)} %bitcast.66, bf16[16,16,128,256]{3,2,1,0:T(8,128)(2,1)} %bitcast.67), kind=kOutput, calls=%fused_computation.18 | convolution fusion | flops 2148007936 | bytes 27262976 | tf_op jit(solution)/shard_map/rtij,rtjc->ric/dot_general | solution.py:37
  226.5 39.1 %psum.23 = f32[256]{0:T(256)S(1)} all-reduce(f32[256]{0:T(256)S(1)} %multiply_reduce_fusion), channel_id=1, replica_groups=mesh['vp'=8,'rep'=4] {'vp','rep'}, use_global_device_ids=true, to_apply=%region_5.0 | all-reduce | flops 256 | bytes 2048 | tf_op jit(solution)/shard_map/psum | solution.py:42
  (58 shorter events, 33.2 us)
Async XLA Ops:
  0.0 18.4 %copy-start = (bf16[2048,256]{1,0:T(8,128)(2,1)S(1)}, bf16[2048,256]{1,0:T(8,128)(2,1)}, u32[]{:S(2)}) copy-start(bf16[2048,256]{1,0:T(8,128)(2,1)} %param.4) | copy-start | bytes 3145732
  0.0 18.3 %copy-start.1 = (s32[256]{0:T(256)S(1)}, s32[256]{0:T(256)}, u32[]{:S(2)}) copy-start(s32[256]{0:T(256)} %param.6) | copy-start | bytes 3076
  2.6 27.9 %collective-permute-start.3 = (bf16[4,128,256]{2,1,0:T(8,128)(2,1)S(1)}, bf16[4,128,256]{2,1,0:T(8,128)(2,1)}, u32[]{:S(2)}, u32[]{:S(2)}) collective-permute-start(bf16[4,128,256]{2,1,0:T(8,128)(2,1)S(1)} %gather_fusion.3), channel_id=1, source_target_pairs={{0,28},{1,29},{2,30},{3,31},{4,0},{5,1},{6,2},{7,3},{8,4},{9,5},{1... | collective-permute-start | bytes 786440 | tf_op jit(solution)/shard_map/ppermute | solution.py:14
  11.2 14.4 %collective-permute-start.1 = (bf16[4,128,256]{2,1,0:T(8,128)(2,1)}, bf16[4,128,256]{2,1,0:T(8,128)(2,1)}, u32[]{:S(2)}, u32[]{:S(2)}) collective-permute-start(bf16[4,128,256]{2,1,0:T(8,128)(2,1)} %gather_fusion.1), channel_id=1, source_target_pairs={{0,31},{1,0},{2,1},{3,2},{4,3},{5,4},{6,5},{7,6},{8,7},{9,8},{10,9... | collective-permute-start | bytes 786440 | tf_op jit(solution)/shard_map/ppermute | solution.py:14
  14.3 10.3 %collective-permute-start = (bf16[4,128,256]{2,1,0:T(8,128)(2,1)}, bf16[4,128,256]{2,1,0:T(8,128)(2,1)}, u32[]{:S(2)}, u32[]{:S(2)}) collective-permute-start(bf16[4,128,256]{2,1,0:T(8,128)(2,1)} %gather_fusion), channel_id=1, source_target_pairs={{0,1},{1,2},{2,3},{3,4},{4,5},{5,6},{6,7},{7,8},{8,9},{9,10},{10,1... | collective-permute-start | bytes 786440 | tf_op jit(solution)/shard_map/ppermute | solution.py:14
  16.8 12.8 %collective-permute-start.2 = (bf16[4,128,256]{2,1,0:T(8,128)(2,1)}, bf16[4,128,256]{2,1,0:T(8,128)(2,1)}, u32[]{:S(2)}, u32[]{:S(2)}) collective-permute-start(bf16[4,128,256]{2,1,0:T(8,128)(2,1)} %gather_fusion.2), channel_id=1, source_target_pairs={{0,4},{1,5},{2,6},{3,7},{4,8},{5,9},{6,10},{7,11},{8,12},{9,13},{1... | collective-permute-start | bytes 786440 | tf_op jit(solution)/shard_map/ppermute | solution.py:14
  92.9 18.2 %collective-permute-start.4 = (bf16[4,128,256]{2,1,0:T(8,128)(2,1)}, bf16[4,128,256]{2,1,0:T(8,128)(2,1)}, u32[]{:S(2)}, u32[]{:S(2)}) collective-permute-start(bf16[4,128,256]{2,1,0:T(8,128)(2,1)} %gather_fusion.5), channel_id=1, source_target_pairs={{0,1},{1,2},{2,3},{3,4},{4,5},{5,6},{6,7},{7,8},{8,9},{9,10},{10,1... | collective-permute-start | bytes 786440 | tf_op jit(solution)/shard_map/ppermute | solution.py:14
  95.3 16.7 %collective-permute-start.5 = (bf16[4,128,256]{2,1,0:T(8,128)(2,1)}, bf16[4,128,256]{2,1,0:T(8,128)(2,1)}, u32[]{:S(2)}, u32[]{:S(2)}) collective-permute-start(bf16[4,128,256]{2,1,0:T(8,128)(2,1)} %gather_fusion.6), channel_id=1, source_target_pairs={{0,31},{1,0},{2,1},{3,2},{4,3},{5,4},{6,5},{7,6},{8,7},{9,8},{10,9... | collective-permute-start | bytes 786440 | tf_op jit(solution)/shard_map/ppermute | solution.py:14
  103.2 9.8 %collective-permute-start.6 = (bf16[4,128,256]{2,1,0:T(8,128)(2,1)}, bf16[4,128,256]{2,1,0:T(8,128)(2,1)}, u32[]{:S(2)}, u32[]{:S(2)}) collective-permute-start(bf16[4,128,256]{2,1,0:T(8,128)(2,1)} %gather_fusion.7), channel_id=1, source_target_pairs={{0,4},{1,5},{2,6},{3,7},{4,8},{5,9},{6,10},{7,11},{8,12},{9,13},{1... | collective-permute-start | bytes 786440 | tf_op jit(solution)/shard_map/ppermute | solution.py:14
  106.3 10.7 %collective-permute-start.7 = (bf16[4,128,256]{2,1,0:T(8,128)(2,1)S(1)}, bf16[4,128,256]{2,1,0:T(8,128)(2,1)S(1)}, u32[]{:S(2)}, u32[]{:S(2)}) collective-permute-start(bf16[4,128,256]{2,1,0:T(8,128)(2,1)S(1)} %gather_fusion.8), channel_id=1, source_target_pairs={{0,28},{1,29},{2,30},{3,31},{4,0},{5,1},{6,2},{7,3},{8,4},{9,5},{1... | collective-permute-start | bytes 786440 | tf_op jit(solution)/shard_map/ppermute | solution.py:14
  182.5 18.2 %collective-permute-start.8 = (bf16[4,128,256]{2,1,0:T(8,128)(2,1)}, bf16[4,128,256]{2,1,0:T(8,128)(2,1)}, u32[]{:S(2)}, u32[]{:S(2)}) collective-permute-start(bf16[4,128,256]{2,1,0:T(8,128)(2,1)} %gather_fusion.10), channel_id=1, source_target_pairs={{0,1},{1,2},{2,3},{3,4},{4,5},{5,6},{6,7},{7,8},{8,9},{9,10},{10,1... | collective-permute-start | bytes 786440 | tf_op jit(solution)/shard_map/ppermute | solution.py:14
  185.0 16.7 %collective-permute-start.9 = (bf16[4,128,256]{2,1,0:T(8,128)(2,1)}, bf16[4,128,256]{2,1,0:T(8,128)(2,1)}, u32[]{:S(2)}, u32[]{:S(2)}) collective-permute-start(bf16[4,128,256]{2,1,0:T(8,128)(2,1)} %gather_fusion.11), channel_id=1, source_target_pairs={{0,31},{1,0},{2,1},{3,2},{4,3},{5,4},{6,5},{7,6},{8,7},{9,8},{10,9... | collective-permute-start | bytes 786440 | tf_op jit(solution)/shard_map/ppermute | solution.py:14
  192.1 10.5 %collective-permute-start.10 = (bf16[4,128,256]{2,1,0:T(8,128)(2,1)S(1)}, bf16[4,128,256]{2,1,0:T(8,128)(2,1)}, u32[]{:S(2)}, u32[]{:S(2)}) collective-permute-start(bf16[4,128,256]{2,1,0:T(8,128)(2,1)S(1)} %gather_fusion.12), channel_id=1, source_target_pairs={{0,4},{1,5},{2,6},{3,7},{4,8},{5,9},{6,10},{7,11},{8,12},{9,13},{1... | collective-permute-start | bytes 786440 | tf_op jit(solution)/shard_map/ppermute | solution.py:14
  196.0 9.8 %collective-permute-start.11 = (bf16[4,128,256]{2,1,0:T(8,128)(2,1)}, bf16[4,128,256]{2,1,0:T(8,128)(2,1)S(1)}, u32[]{:S(2)}, u32[]{:S(2)}) collective-permute-start(bf16[4,128,256]{2,1,0:T(8,128)(2,1)} %gather_fusion.13), channel_id=1, source_target_pairs={{0,28},{1,29},{2,30},{3,31},{4,0},{5,1},{6,2},{7,3},{8,4},{9,5},{1... | collective-permute-start | bytes 786440 | tf_op jit(solution)/shard_map/ppermute | solution.py:14
where the time goes:
time: 268 us; the launch traced here: 267 us
  blocking collectives  117 us (44%)
  local copies, waits for them, and re-layouts  69.5 us (26%)
  matrix products  31.5 us (12%)
  starting transfers between devices  28.4 us (11%)
  waiting for transfers between devices  14.1 us (5%)
  other arithmetic  6.05 us (2%)
    psum x3, blocking collectives, local(): total_mass = lax.psum(local_mass, ('vp', 'rep'))  117 us
    dot_general x3, matrix products, local(): jnp.einsum('rtij,rtjc->ric', tiles, picked, preferred_element_type=jnp.fl...  31.5 us
    gather x3, local copies, waits for them, and re-layouts, local(): picked = block_table[tile_slots]  29.2 us
    ppermute x12, starting transfers between devices, passed_along(): lax.ppermute(shard, axis, [(i, (i + by) % count) for i in range(count)])  28.4 us
    gather x12, local copies, waits for them, and re-layouts, local(): own_blocks[send_lists[which]]  27.8 us
    ppermute x12, waiting for transfers between devices, passed_along(): lax.ppermute(shard, axis, [(i, (i + by) % count) for i in range(count)])  14.1 us
    unnamed x16, local copies, waits for them, and re-layouts  11.4 us
  transfers between devices with their start and end apart: 12, of which 4 were waited for; matrix products, arithmetic and copies ran while one was open for 12% of the time, Pallas kernels for 0%

commit v1 on v0

v1 whole, which is shorter than its diff:
```python
import functools

import jax
import jax.numpy as jnp
from jax import lax
from jax.experimental import pallas as pl
from jax.experimental.pallas import tpu as pltpu
from jax.sharding import PartitionSpec as P

ITERS = 3
LANES = 128
OFFSETS = (1, -1, 4, -4)
MESH = pl.DeviceIdType.MESH
LOADS = 8


def kernel(vp_count, rep_count, vertices, slots, halves, *refs):
    cols_ref, rows_ref, feat_hbm, tiles_hbm, out_hbm = refs[:5]
    it_refs = iter(refs[5:])
    take = lambda count: [next(it_refs) for _ in range(count)]
    tiles = take(1)[0]
    tables = [take(halves) for _ in range(ITERS)]
    feats = take(halves)
    owns = take(halves)
    sends = [take(halves) for _ in range(ITERS)]
    finals = take(halves)
    stages = take(halves)
    mine_a = [take(halves) for _ in range(ITERS)]
    got_a = [take(halves) for _ in range(ITERS)]
    mine_b = [take(halves) for _ in range(ITERS)]
    got_b = [take(halves) for _ in range(ITERS)]
    (tile_sem, feat_sem, table_sem, out_sem, send_sem, recv_sem,
     a_send, a_recv, b_send, b_recv) = take(10)

    nblocks, tile_size = feats[0].shape[0], feats[0].shape[1]
    ntiles = tiles.shape[0]
    per_row = ntiles // nblocks
    my_vp, my_rep = lax.axis_index("vp"), lax.axis_index("rep")
    me = my_vp * rep_count + my_rep
    shards = vp_count * rep_count

    own_loads, table_loads = [], []
    for h in range(halves):
        part = feat_hbm.at[:, :, pl.ds(h * LANES, LANES)]
        own_loads.append(pltpu.make_async_copy(part, feats[h], feat_sem.at[h]))
        table_loads.append(
            pltpu.make_async_copy(part, tables[0][h].at[pl.ds(0, nblocks)], table_sem.at[h])
        )
    for h in range(halves):
        own_loads[h].start()
    for h in range(halves):
        table_loads[h].start()
    chunk = ntiles // LOADS
    tile_loads = []
    for k in range(LOADS):
        piece = pl.ds(k * chunk, chunk)
        tile_loads.append(pltpu.make_async_copy(tiles_hbm.at[piece], tiles.at[piece], tile_sem.at[k]))
        tile_loads[-1].start()

    peers = []
    for off in OFFSETS:
        flat = lax.rem(me + off + shards, shards)
        peers.append((flat // rep_count, lax.rem(flat, rep_count)))
    rep_peers = [(my_vp, lax.rem(my_rep + k, rep_count)) for k in range(1, rep_count)]
    vp_peers = [(lax.rem(my_vp + k, vp_count), my_rep) for k in range(1, vp_count)]
    everyone = peers + rep_peers + vp_peers
    barrier = pltpu.get_barrier_semaphore()
    for peer in everyone:
        pl.semaphore_signal(barrier, inc=1, device_id=peer, device_id_type=MESH)
    pl.semaphore_wait(barrier, len(everyone))

    def halo_copy(it, h, o):
        at = (it * halves + h) * 4 + o
        return pltpu.make_async_remote_copy(
            src_ref=sends[it][h].at[pl.ds(o * slots, slots)],
            dst_ref=tables[it][h].at[pl.ds(nblocks + o * slots, slots)],
            send_sem=send_sem.at[at],
            recv_sem=recv_sem.at[at],
            device_id=peers[o],
            device_id_type=MESH,
        )

    def send_halo(it, h, source):
        for k in range(4 * slots):
            sends[it][h][k] = source[rows_ref[k]]
        for o in (2, 3, 0, 1):
            halo_copy(it, h, o).start()

    def mass_copy(it, h, k, mine, got, s_sem, r_sem, group):
        at = (it * halves + h) * len(group) + k
        return pltpu.make_async_remote_copy(
            src_ref=mine[it][h],
            dst_ref=got[it][h].at[k],
            send_sem=s_sem.at[at],
            recv_sem=r_sem.at[at],
            device_id=group[k],
            device_id_type=MESH,
        )

    def copies_a(it, h):
        return [mass_copy(it, h, k, mine_a, got_a, a_send, a_recv, rep_peers) for k in range(len(rep_peers))]

    def copies_b(it, h):
        return [mass_copy(it, h, k, mine_b, got_b, b_send, b_recv, vp_peers) for k in range(len(vp_peers))]

    def mass_first(it, h, mass):
        mine_a[it][h][...] = mass
        for copy in copies_a(it, h):
            copy.start()

    def mass_second(it, h):
        for copy in copies_a(it, h):
            copy.wait_recv()
        mine_b[it][h][...] = mine_a[it][h][...] + jnp.sum(got_a[it][h][...], axis=0)
        for copy in copies_b(it, h):
            copy.start()

    def mass_total(it, h):
        for copy in copies_b(it, h):
            copy.wait_recv()
        total = mine_b[it][h][...] + jnp.sum(got_b[it][h][...], axis=0)
        return 1.0 / jnp.sqrt(0.05 + total / vertices)

    def propagate(it, h, gain):
        table = tables[it][h]

        def row(r, mass):
            first = r * per_row
            left = jnp.concatenate([tiles[first + t] for t in range(per_row)], axis=1)
            right = jnp.concatenate([table[cols_ref[first + t]] for t in range(per_row)], axis=0)
            total = jnp.dot(left, right, preferred_element_type=jnp.float32)
            blended = gain * total + 0.1 * feats[h][r].astype(jnp.float32)
            if it + 1 < ITERS:
                rounded = blended.astype(jnp.bfloat16)
                owns[h][r] = rounded
                tables[it + 1][h][r] = rounded
            else:
                finals[h][r] = blended
            squares = (blended * blended).reshape(tile_size // 8, 8, LANES)
            return mass + jnp.sum(squares, axis=0)

        mass = lax.fori_loop(0, nblocks, row, jnp.zeros((8, LANES), jnp.float32))
        return jnp.sum(mass, axis=0, keepdims=True)

    for h in range(halves):
        own_loads[h].wait()
        send_halo(0, h, feats[h])
    for h in range(halves):
        table_loads[h].wait()
    for load in tile_loads:
        load.wait()

    def finish(h):
        scale = mass_total(ITERS - 1, h)
        for b in range(nblocks):
            stages[h][b] = (finals[h][b] * scale).astype(jnp.bfloat16)
        pltpu.make_async_copy(
            stages[h], out_hbm.at[:, :, pl.ds(h * LANES, LANES)], out_sem.at[h]
        ).start()

    for it in range(ITERS):
        for h in range(halves):
            for o in range(4):
                halo_copy(it, h, o).wait_recv()
            gain = 0.9 if it == 0 else 0.9 * mass_total(it - 1, h)
            mass = propagate(it, h, gain)
            mass_first(it, h, mass)
            if it + 1 < ITERS:
                send_halo(it + 1, h, owns[h])
            mass_second(it, h)
    for h in range(halves):
        finish(h)
    for it in range(ITERS):
        for h in range(halves):
            for o in range(4):
                halo_copy(it, h, o).wait_send()
            for copy in copies_a(it, h) + copies_b(it, h):
                copy.wait_send()
    for h in range(halves):
        pltpu.make_async_copy(
            stages[h], out_hbm.at[:, :, pl.ds(h * LANES, LANES)], out_sem.at[h]
        ).wait()


def local(vp_count, rep_count, features, tile_values, tile_cols, halo_rows):
    tile_size = tile_values.shape[1]
    rows, classes = features.shape
    nblocks = rows // tile_size
    slots = halo_rows.shape[2]
    halves = classes // LANES
    shards = vp_count * rep_count
    block = (tile_size, LANES)
    bf16, f32 = jnp.bfloat16, jnp.float32
    each = ITERS * halves
    scratch = [pltpu.VMEM(tile_values.shape, bf16)]
    scratch += [pltpu.VMEM((nblocks + 4 * slots,) + block, bf16)] * each
    scratch += [pltpu.VMEM((nblocks,) + block, bf16)] * (2 * halves)
    scratch += [pltpu.VMEM((4 * slots,) + block, bf16)] * each
    scratch += [pltpu.VMEM((nblocks,) + block, f32)] * halves
    scratch += [pltpu.VMEM((nblocks,) + block, bf16)] * halves
    scratch += [pltpu.VMEM((1, LANES), f32)] * each
    scratch += [pltpu.VMEM((rep_count - 1, 1, LANES), f32)] * each
    scratch += [pltpu.VMEM((1, LANES), f32)] * each
    scratch += [pltpu.VMEM((vp_count - 1, 1, LANES), f32)] * each
    dma = lambda count: pltpu.SemaphoreType.DMA((count,))
    scratch += [dma(LOADS), dma(halves), dma(halves), dma(halves), dma(each * 4), dma(each * 4)]
    scratch += [dma(each * (rep_count - 1))] * 2 + [dma(each * (vp_count - 1))] * 2
    out = pl.pallas_call(
        functools.partial(kernel, vp_count, rep_count, rows * shards, slots, halves),
        out_shape=jax.ShapeDtypeStruct((nblocks, tile_size, classes), bf16),
        in_specs=[pl.BlockSpec(memory_space=pltpu.SMEM)] * 2
        + [pl.BlockSpec(memory_space=pl.ANY)] * 2,
        out_specs=pl.BlockSpec(memory_space=pl.ANY),
        scratch_shapes=scratch,
        compiler_params=pltpu.CompilerParams(
            collective_id=0, has_side_effects=True, vmem_limit_bytes=60 * 1024 * 1024
        ),
    )(tile_cols, halo_rows.reshape(-1), features.reshape(nblocks, tile_size, classes), tile_values)
    return out.reshape(rows, classes)


def solution(mesh):
    return jax.shard_map(
        functools.partial(local, mesh.shape["vp"], mesh.shape["rep"]),
        mesh=mesh,
        in_specs=(
            P(("vp", "rep"), None),
            P(("vp", "rep"), None, None),
            P(("vp", "rep")),
            P(("vp", "rep"), None, None),
        ),
        out_specs=P(("vp", "rep"), None),
        check_vma=False,
    )
```

time: 268 us -> 77.6 us (0.29)
  blocking collectives: 117 us -> 0 us
  Pallas kernels: 0 us -> 73.9 us
  local copies, waits for them, and re-layouts: 69.5 us -> 3.54 us
  matrix products: 31.5 us -> 0 us
  starting transfers between devices: 28.4 us -> 0 us
  waiting for transfers between devices: 14.1 us -> 0 us
  other arithmetic: 6.05 us -> 0 us
    psum x3 -> x0, blocking collectives: 117 us -> none  [local(): total_mass = lax.psum(local_mass, ('vp', 'rep'))]
    pallas_call x0 -> x1, Pallas kernels: none -> 73.9 us  [local(): pl.pallas_call(functools.partial(kernel, vp_count, rep_count, rows * shar...]
    gather x15 -> x0, local copies, waits for them, and re-layouts: 57 us -> none  [the longest x3 29.2 us: local(): picked = block_table[tile_slots]]
    dot_general x3 -> x0, matrix products: 31.5 us -> none  [local(): jnp.einsum('rtij,rtjc->ric', tiles, picked, preferred_element_type=jnp.fl...]
    ppermute x12 -> x0, starting transfers between devices: 28.4 us -> none  [passed_along(): lax.ppermute(shard, axis, [(i, (i + by) % count) for i in range(count)])]
    ppermute x12 -> x0, waiting for transfers between devices: 14.1 us -> none  [passed_along(): lax.ppermute(shard, axis, [(i, (i + by) % count) for i in range(count)])]
    unnamed x16 -> x1, local copies, waits for them, and re-layouts: 11.4 us -> 2.26 us
    convert_element_type x3 -> x0, other arithmetic: 3.89 us -> none  [local(): (blended / jnp.sqrt(0.05 + total_mass / vertices)).astype(jnp.bfloat16)]
  transfers between devices with their start and end apart: 12 -> 0, of which waited for: 4 -> 0; matrix products, arithmetic and copies ran while one was open for 12% -> 0% of each run, Pallas kernels for 0% -> 0%
where the time goes in v1:
time: 77.6 us; the launch traced here: 77.4 us
  Pallas kernels  73.9 us (95%)
  local copies, waits for them, and re-layouts  3.54 us (5%)
    pallas_call x1, Pallas kernels, local(): pl.pallas_call(functools.partial(kernel, vp_count, rep_count, rows * shar...  73.9 us
    unnamed x1, local copies, waits for them, and re-layouts  2.26 us

profile of v1, /device:TPU:0, one launch (start us, length us, event | category | flops | bytes accessed | tf_op | source)
XLA Modules:
  0.0 77.4 jit_solution(14934945893059432419)
XLA Ops:
  0.0 1.3 %reshape.9.refs_1_ = s32[16]{0:T(128)} reshape(s32[1,4,4]{2,1,0:T(4,128)} %param.7) | data formatting | bytes 128 | tf_op jit(solution)/shard_map/reshape | solution.py:218
  1.3 73.9 %shard_map.46 = bf16[16,128,256]{2,1,0:T(8,128)(2,1)} custom-call(s32[256]{0:T(256)} %refs_0_.1, s32[16]{0:T(128)} %reshape.9.refs_1_, bf16[16,128,256]{2,1,0:T(8,128)(2,1)} %bitcast.3, bf16[256,128,128]{2,1,0:T(8,128)(2,1)} %refs_3_.1), custom_call_target="tpu_custom_call" | custom-call | tf_op jit(solution)/shard_map/pallas_call | solution.py:208
  75.2 2.3 %copy.6 = bf16[2048,256]{1,0:T(8,128)(2,1)} copy(bf16[2048,256]{1,0:T(8,128)(2,1)} %bitcast.2) | data formatting | bytes 2097152

commit v2 on v1

v2 whole, which is shorter than its diff:
```python
import functools

import jax
import jax.numpy as jnp
from jax import lax
from jax.experimental import pallas as pl
from jax.experimental.pallas import tpu as pltpu
from jax.sharding import PartitionSpec as P

ITERS = 3
LANES = 128
MESH = pl.DeviceIdType.MESH
LOADS = 8


def kernel(vp_count, rep_count, vertices, slots, halves, *refs):
    cols_ref, rows_ref, feat_hbm, tiles_hbm, out_hbm = refs[:5]
    it_refs = iter(refs[5:])
    take = lambda count: [next(it_refs) for _ in range(count)]
    tiles = take(1)[0]
    tables = [take(halves) for _ in range(ITERS)]
    feats = take(halves)
    owns = take(halves)
    sends = [take(halves) for _ in range(ITERS)]
    finals = take(halves)
    stages = take(halves)
    mine = [take(halves) for _ in range(ITERS)]
    got = [take(halves) for _ in range(ITERS)]
    order, place = take(2)
    (tile_sem, feat_sem, table_sem, out_sem, send_sem, recv_sem, mass_send, mass_recv) = take(8)

    nblocks, tile_size = feats[0].shape[0], feats[0].shape[1]
    ntiles = tiles.shape[0]
    per_row = ntiles // nblocks
    my_vp, my_rep = lax.axis_index("vp"), lax.axis_index("rep")
    me = my_vp * rep_count + my_rep
    shards = vp_count * rep_count

    own_loads, table_loads = [], []
    for h in range(halves):
        part = feat_hbm.at[:, :, pl.ds(h * LANES, LANES)]
        own_loads.append(pltpu.make_async_copy(part, feats[h], feat_sem.at[h]))
        table_loads.append(
            pltpu.make_async_copy(part, tables[0][h].at[pl.ds(0, nblocks)], table_sem.at[h])
        )
    for h in range(halves):
        own_loads[h].start()
    for h in range(halves):
        table_loads[h].start()
    chunk = ntiles // LOADS
    tile_loads = []
    for k in range(LOADS):
        piece = pl.ds(k * chunk, chunk)
        tile_loads.append(pltpu.make_async_copy(tiles_hbm.at[piece], tiles.at[piece], tile_sem.at[k]))
        tile_loads[-1].start()

    def device_at(distance):
        flat = lax.rem(me + distance + shards, shards)
        return flat // rep_count, lax.rem(flat, rep_count)

    def peer_at(o):
        size = 1 + 3 * (o // 2)
        return device_at(size * (1 - 2 * lax.rem(o, 2)))

    barrier = pltpu.get_barrier_semaphore()

    def greet(k, carry):
        pl.semaphore_signal(barrier, inc=1, device_id=device_at(k), device_id_type=MESH)
        return carry

    lax.fori_loop(1, shards, greet, 0)

    def sent(o, j):
        return rows_ref[0, o, j]

    turns = []
    for b in range(nblocks):
        turn = jnp.int32(4)
        for g in reversed(range(4)):
            hit = sent((g + 2) % 4, 0) == b
            for j in range(1, slots):
                hit = hit | (sent((g + 2) % 4, j) == b)
            turn = jnp.where(hit, g, turn)
        turns.append(turn * nblocks + b)
    places = []
    for b in range(nblocks):
        at = jnp.int32(0)
        for c in range(nblocks):
            if c != b:
                at = at + jnp.where(turns[c] < turns[b], 1, 0)
        places.append(at)
        place[b] = at
    for b in range(4 * slots):
        place[nblocks + b] = jnp.int32(nblocks + b)
    for k in range(nblocks):
        row = jnp.int32(0)
        for b in range(nblocks):
            row = row + jnp.where(places[b] == k, b, 0)
        order[k] = row

    pl.semaphore_wait(barrier, shards - 1)

    def halo_copy(it, h, o):
        at = (it * halves + h) * 4 + o
        return pltpu.make_async_remote_copy(
            src_ref=sends[it][h].at[pl.ds(o * slots, slots)],
            dst_ref=tables[it][h].at[pl.ds(nblocks + o * slots, slots)],
            send_sem=send_sem.at[at],
            recv_sem=recv_sem.at[at],
            device_id=peer_at(o),
            device_id_type=MESH,
        )

    def send_halo(it, h, o, source):
        for j in range(slots):
            row = rows_ref[0, o, j]
            sends[it][h][o * slots + j] = source[place[row] if it else row]
        halo_copy(it, h, o).start()

    def mass_copy(it, h, k):
        at = it * halves + h
        return pltpu.make_async_remote_copy(
            src_ref=mine[it][h],
            dst_ref=got[it][h].at[k - 1],
            send_sem=mass_send.at[at, k - 1],
            recv_sem=mass_recv.at[at, k - 1],
            device_id=device_at(k),
            device_id_type=MESH,
        )

    def each_other(it, h, act):
        def one(k, carry):
            act(mass_copy(it, h, k))
            return carry

        lax.fori_loop(1, shards, one, 0)

    def mass_first(it, h, mass):
        mine[it][h][...] = mass
        each_other(it, h, lambda copy: copy.start())

    def mass_total(it, h):
        each_other(it, h, lambda copy: copy.wait_recv())
        total = mine[it][h][...] + jnp.sum(got[it][h][...], axis=0)
        return 1.0 / jnp.sqrt(0.05 + total / vertices)

    def propagate(it, h, gain):
        table = tables[it][h]
        last = it + 1 == ITERS

        def row(k, mass):
            r = k if last else order[k]
            first = r * per_row
            slot = lambda t: cols_ref[first + t]
            source = slot if it == 0 else lambda t: place[slot(t)]
            left = jnp.concatenate([tiles[first + t] for t in range(per_row)], axis=1)
            right = jnp.concatenate([table[source(t)] for t in range(per_row)], axis=0)
            total = jnp.dot(left, right, preferred_element_type=jnp.float32)
            blended = gain * total + 0.1 * feats[h][r].astype(jnp.float32)
            if last:
                finals[h][k] = blended
            else:
                rounded = blended.astype(jnp.bfloat16)
                owns[h][k] = rounded
                tables[it + 1][h][k] = rounded
            squares = (blended * blended).reshape(tile_size // 8, 8, LANES)
            return mass + jnp.sum(squares, axis=0)

        def group(g, mass):
            for k in range(nblocks // 4):
                mass = row(g * (nblocks // 4) + k, mass)
            if not last:
                send_halo(it + 1, h, lax.rem(g + 2, 4), owns[h])
            return mass

        mass = lax.fori_loop(0, 4, group, jnp.zeros((8, LANES), jnp.float32))
        return jnp.sum(mass, axis=0, keepdims=True)

    for h in range(halves):
        own_loads[h].wait()
        for o in (2, 3, 0, 1):
            send_halo(0, h, o, feats[h])
    for h in range(halves):
        table_loads[h].wait()
    for load in tile_loads:
        load.wait()

    def finish(h):
        scale = mass_total(ITERS - 1, h)
        for b in range(nblocks):
            stages[h][b] = (finals[h][b] * scale).astype(jnp.bfloat16)
        pltpu.make_async_copy(
            stages[h], out_hbm.at[:, :, pl.ds(h * LANES, LANES)], out_sem.at[h]
        ).start()

    for it in range(ITERS):
        for h in range(halves):
            for o in range(4):
                halo_copy(it, h, o).wait_recv()
            gain = 0.9 if it == 0 else 0.9 * mass_total(it - 1, h)
            mass = propagate(it, h, gain)
            mass_first(it, h, mass)
    for h in range(halves):
        finish(h)
    for it in range(ITERS):
        for h in range(halves):
            for o in range(4):
                halo_copy(it, h, o).wait_send()
            each_other(it, h, lambda copy: copy.wait_send())
    for h in range(halves):
        pltpu.make_async_copy(
            stages[h], out_hbm.at[:, :, pl.ds(h * LANES, LANES)], out_sem.at[h]
        ).wait()


def local(vp_count, rep_count, features, tile_values, tile_cols, halo_rows):
    tile_size = tile_values.shape[1]
    rows, classes = features.shape
    nblocks = rows // tile_size
    slots = halo_rows.shape[2]
    halves = classes // LANES
    shards = vp_count * rep_count
    block = (tile_size, LANES)
    bf16, f32 = jnp.bfloat16, jnp.float32
    each = ITERS * halves
    scratch = [pltpu.VMEM(tile_values.shape, bf16)]
    scratch += [pltpu.VMEM((nblocks + 4 * slots,) + block, bf16)] * each
    scratch += [pltpu.VMEM((nblocks,) + block, bf16)] * (2 * halves)
    scratch += [pltpu.VMEM((4 * slots,) + block, bf16)] * each
    scratch += [pltpu.VMEM((nblocks,) + block, f32)] * halves
    scratch += [pltpu.VMEM((nblocks,) + block, bf16)] * halves
    scratch += [pltpu.VMEM((1, LANES), f32)] * each
    scratch += [pltpu.VMEM((shards - 1, 1, LANES), f32)] * each
    scratch += [pltpu.SMEM((nblocks,), jnp.int32), pltpu.SMEM((nblocks + 4 * slots,), jnp.int32)]
    dma = lambda *shape: pltpu.SemaphoreType.DMA(shape)
    scratch += [dma(LOADS), dma(halves), dma(halves), dma(halves), dma(each * 4), dma(each * 4)]
    scratch += [dma(each, shards - 1)] * 2
    out = pl.pallas_call(
        functools.partial(kernel, vp_count, rep_count, rows * shards, slots, halves),
        out_shape=jax.ShapeDtypeStruct((nblocks, tile_size, classes), bf16),
        in_specs=[pl.BlockSpec(memory_space=pltpu.SMEM)] * 2
        + [pl.BlockSpec(memory_space=pl.ANY)] * 2,
        out_specs=pl.BlockSpec(memory_space=pl.ANY),
        scratch_shapes=scratch,
        compiler_params=pltpu.CompilerParams(
            collective_id=0, has_side_effects=True, vmem_limit_bytes=60 * 1024 * 1024
        ),
    )(tile_cols, halo_rows, features.reshape(nblocks, tile_size, classes), tile_values)
    return out.reshape(rows, classes)


def solution(mesh):
    return jax.shard_map(
        functools.partial(local, mesh.shape["vp"], mesh.shape["rep"]),
        mesh=mesh,
        in_specs=(
            P(("vp", "rep"), None),
            P(("vp", "rep"), None, None),
            P(("vp", "rep")),
            P(("vp", "rep"), None, None),
        ),
        out_specs=P(("vp", "rep"), None),
        check_vma=False,
    )
```

time: 77.6 us -> 69.9 us (0.901)
  Pallas kernels: 73.9 us -> 67.4 us
  local copies, waits for them, and re-layouts: 3.54 us -> 2.26 us
    pallas_call x1, Pallas kernels: 73.9 us -> 67.4 us  [local(): pl.pallas_call(functools.partial(kernel, vp_count, rep_count, rows * shar...]
    reshape x1 -> x0, local copies, waits for them, and re-layouts: 1.27 us -> none  [local(): halo_rows.reshape(-1)]
where the time goes in v2:
time: 69.9 us; the launch traced here: 69.7 us
  Pallas kernels  67.4 us (96%)
  local copies, waits for them, and re-layouts  2.26 us (3%)
    pallas_call x1, Pallas kernels, local(): pl.pallas_call(functools.partial(kernel, vp_count, rep_count, rows * shar...  67.4 us
    unnamed x1, local copies, waits for them, and re-layouts  2.26 us

profile of v2, /device:TPU:0, one launch (start us, length us, event | category | flops | bytes accessed | tf_op | source)
XLA Modules:
  0.0 69.7 jit_solution(6428613289086901377)
XLA Ops:
  0.0 67.4 %shard_map.46 = bf16[16,128,256]{2,1,0:T(8,128)(2,1)} custom-call(s32[256]{0:T(256)} %refs_0_.1, s32[1,4,4]{2,1,0:T(4,128)} %refs_1_.1, bf16[16,128,256]{2,1,0:T(8,128)(2,1)} %bitcast.3, bf16[256,128,128]{2,1,0:T(8,128)(2,1)} %refs_3_.1), custom_call_target="tpu_custom_call" | custom-call | tf_op jit(solution)/shard_map/pallas_call | solution.py:238
  67.4 2.3 %copy.6 = bf16[2048,256]{1,0:T(8,128)(2,1)} copy(bf16[2048,256]{1,0:T(8,128)(2,1)} %bitcast.2) | data formatting | bytes 2097152

commit v3 on v2

--- a/solution.py
+++ b/solution.py
@@ -11,6 +11,7 @@
 LANES = 128
 MESH = pl.DeviceIdType.MESH
 LOADS = 8
+UNROLL = 64
 
 
 def kernel(vp_count, rep_count, vertices, slots, halves, *refs):
@@ -133,7 +134,7 @@
             act(mass_copy(it, h, k))
             return carry
 
-        lax.fori_loop(1, shards, one, 0)
+        lax.fori_loop(1, shards, one, 0, unroll=shards <= UNROLL)
 
     def mass_first(it, h, mass):
         mine[it][h][...] = mass

time: 69.9 us -> 69.2 us (0.990)
  no operation moved by 1% of the time
where the time goes in v3:
time: 69.2 us; the launch traced here: 69 us
  Pallas kernels  66.8 us (97%)
  local copies, waits for them, and re-layouts  2.26 us (3%)
    pallas_call x1, Pallas kernels, local(): pl.pallas_call(functools.partial(kernel, vp_count, rep_count, rows * shar...  66.8 us
    unnamed x1, local copies, waits for them, and re-layouts  2.26 us

profile of v3, /device:TPU:0, one launch (start us, length us, event | category | flops | bytes accessed | tf_op | source)
XLA Modules:
  0.0 69.0 jit_solution(8555206069593556239)
XLA Ops:
  0.0 66.8 %shard_map.46 = bf16[16,128,256]{2,1,0:T(8,128)(2,1)} custom-call(s32[256]{0:T(256)} %refs_0_.1, s32[1,4,4]{2,1,0:T(4,128)} %refs_1_.1, bf16[16,128,256]{2,1,0:T(8,128)(2,1)} %bitcast.3, bf16[256,128,128]{2,1,0:T(8,128)(2,1)} %refs_3_.1), custom_call_target="tpu_custom_call" | custom-call | tf_op jit(solution)/shard_map/pallas_call | solution.py:239
  66.8 2.3 %copy.6 = bf16[2048,256]{1,0:T(8,128)(2,1)} copy(bf16[2048,256]{1,0:T(8,128)(2,1)} %bitcast.2) | data formatting | bytes 2097152
